TPU v7x, 32 devices: a whole 2x2x4 slice. The times are simulated.
32 devices in a mesh: dp: 16 (over z, y, x), tensor: 2 (over core).
Axes of the slice: x: 2, y: 2, z: 4, core: 2. Of those that a mesh axis runs over, the one named last changes fastest.
Arguments:
- hidden: bfloat16 [16384, 7168], P('dp', 'tensor'), parts along dimension 0, may hold values from -6 to 6
- w_dq: bfloat16 [7168, 1536], P('tensor'), may hold values from -0.0625 to 0.0625
- w_dkv: bfloat16 [7168, 576], P('tensor'), may hold values from -0.0625 to 0.0625
- q_gain: float32 [1536], replicated, may hold values from 0.1 to 1.9
- kv_gain: float32 [512], replicated, may hold values from 0.1 to 1.9
- w_uq: bfloat16 [1536, 12288], P(None, 'tensor'), may hold values from -0.15625 to 0.15625
- w_ukv: bfloat16 [512, 16384], P(None, 'tensor'), may hold values from -0.25 to 0.25
Outputs:
- queries: bfloat16 [16384, 12288], P('dp', 'tensor'), parts along dimension 0
- keys_values: bfloat16 [16384, 16384], P('dp', 'tensor'), parts along dimension 0
- rotary_key: bfloat16 [16384, 64], P(('dp', 'tensor')), parts along dimension 0
There are 16 independent parts, one for each index of `dp`. A program takes and returns all parts, laid end to end along the dimension named above; an argument that names none is the same for every part. Nothing has to cross between parts.
All inputs are finite; a program needn't handle non-finite values.
Results may differ from a plain program's by a relative error of at most 0.0049.
Values may be sent and summed in bfloat16 or wider, within the bound.
A program may use at most 192 MiB of HBM per device.

v0:
```python
import jax
import jax.numpy as jnp
from jax import lax
from jax.sharding import PartitionSpec as P

NOPE = 128
ROPE = 64


def rotate(values, angle):
    half = values.shape[-1] // 2
    first = values[..., :half]
    second = values[..., half:]
    cosine = jnp.cos(angle)
    sine = jnp.sin(angle)
    return jnp.concatenate(
        [first * cosine - second * sine, second * cosine + first * sine], axis=-1
    )


def angles(first_row, count, half):
    positions = (first_row + lax.iota(jnp.int32, count)).astype(jnp.float32)
    freqs = 50000.0 ** (-jnp.arange(half, dtype=jnp.float32) / half)
    return positions[:, None] * freqs[None, :]


def normalize(block, gain):
    scale = lax.rsqrt(jnp.mean(block * block, axis=1, keepdims=True) + 1e-06)
    return (block * scale * gain[None, :]).astype(jnp.bfloat16)


def shards(hidden, w_dq, w_dkv, q_gain, kv_gain, w_uq, w_ukv):
    q_width = w_dq.shape[1]
    kv_width = kv_gain.shape[0]
    rope_width = w_dkv.shape[1] - kv_width
    head_width = NOPE + ROPE
    local_heads = w_uq.shape[1] // head_width
    total_rows = hidden.shape[0]
    share = total_rows // lax.axis_size("tensor")
    own_start = lax.axis_index("tensor") * share
    down = lax.psum_scatter(
        jnp.concatenate(
            [
                jnp.dot(hidden, w_dq, preferred_element_type=jnp.float32),
                jnp.dot(hidden, w_dkv, preferred_element_type=jnp.float32),
            ],
            axis=1,
        ),
        "tensor",
        scatter_dimension=0,
        tiled=True,
    )
    latent = jnp.concatenate(
        [
            normalize(down[:, :q_width], q_gain),
            normalize(down[:, q_width : q_width + kv_width], kv_gain),
        ],
        axis=1,
    )
    piece = lax.all_gather(latent, "tensor", axis=0, tiled=True)
    count = piece.shape[0]
    query_full = jnp.dot(piece[:, :q_width], w_uq, preferred_element_type=jnp.float32)
    query_full = query_full.reshape(count, local_heads, head_width)
    angle = angles(jnp.int32(0), count, ROPE // 2)
    turned = rotate(query_full[:, :, NOPE:], angle[:, None, :])
    query_out = jnp.concatenate([query_full[:, :, :NOPE], turned], axis=2)
    query_out = query_out.reshape(count, local_heads * head_width).astype(jnp.bfloat16)
    kv_out = jnp.dot(piece[:, q_width:], w_ukv, preferred_element_type=jnp.float32).astype(
        jnp.bfloat16
    )
    both = jnp.concatenate([query_out, kv_out], axis=1)
    mine = down[:, q_width + kv_width :]
    rotary_key = rotate(mine, angles(own_start, share, rope_width // 2)).astype(jnp.bfloat16)
    query_cols = local_heads * head_width
    return (both[:, :query_cols], both[:, query_cols:], rotary_key)


def solution(mesh):
    in_specs = (
        P("dp", "tensor"),
        P("tensor", None),
        P("tensor", None),
        P(),
        P(),
        P(None, "tensor"),
        P(None, "tensor"),
    )
    out_specs = (P("dp", "tensor"), P("dp", "tensor"), P(("dp", "tensor"), None))
    return jax.shard_map(shards, mesh=mesh, in_specs=in_specs, out_specs=out_specs, check_vma=False)
```

profile of v0, /device:TPU:13, one launch (start us, length us, event | category | flops | bytes accessed | tf_op | source)
XLA Modules:
  0.0 163.9 jit_solution(327026289376337164)
XLA Ops:
  7.2 0.0 reduce-scatter.2.cloned.1.call-start
  7.2 0.0 copy-start.2
  7.2 16.7 %fusion.11 = f32[1024,1536]{0,1:T(8,128)S(1)} fusion(bf16[1024,3584]{1,0:T(8,128)(2,1)} %param.7, bf16[3584,1536]{1,0:T(8,128)(2,1)} %param.8), kind=kOutput, calls=%fused_computation.32 | convolution fusion | flops 11274289152 | bytes 24641536 | tf_op jit(solution)/shard_map/dot_general | solution.py:44
  23.9 0.0 copy-done.2
  24.0 6.7 %fusion.12 = f32[1024,576]{0,1:T(8,128)S(1)} fusion(bf16[1024,3584]{1,0:T(8,128)(2,1)} %param.7, bf16[3584,576]{0,1:T(8,128)(2,1)S(1)} %copy-done.2), kind=kOutput, calls=%fused_computation.33 | convolution fusion | flops 4227858432 | bytes 13828096 | tf_op jit(solution)/shard_map/dot_general | solution.py:45
  30.7 4.6 %pad_maximum_fusion.1 = f32[1024,2112]{0,1:T(8,128)} fusion(f32[1024,576]{0,1:T(8,128)S(1)} %fusion.12, f32[1024,1536]{0,1:T(8,128)S(1)} %fusion.11), kind=kLoop, calls=%fused_computation.3 | loop fusion | flops 2162688 | bytes 17301504 | tf_op jit(solution)/shard_map/concatenate | solution.py:42
  35.3 0.0 copy-start
  35.3 0.0 reduce-scatter.2.cloned.1.call-update
  35.3 0.0 copy-start.1
  35.3 0.2 all-gather.2.cloned.1.call-start
  35.6 18.2 %reduce-scatter.2.cloned.1.call-done = f32[512,2112]{0,1:T(8,128)} async-done(((f32[1024,2112]{0,1:T(8,128)}), f32[512,2112]{0,1:T(8,128)}) %reduce-scatter.2.cloned.1.call-update) | async-done | bytes 4325392 | tf_op jit(solution)/shard_map/reduce_scatter | solution.py:41
  53.7 2.2 %multiply_reduce_fusion = f32[512]{0:T(512)S(1)} fusion(f32[512,2112]{0,1:T(8,128)} %reduce-scatter.2.cloned.1.call-done), kind=kLoop, calls=%fused_computation.9 | loop fusion | flops 1572352 | bytes 3147776 | tf_op jit(solution)/shard_map/reduce_sum | solution.py:28
  55.9 1.3 multiply_reduce_fusion.1
  57.2 0.0 copy-done
  57.3 2.2 %multiply_convert_fusion = bf16[512,1536]{0,1:T(8,128)(2,1)S(1)} fusion(f32[512,2112]{0,1:T(8,128)} %reduce-scatter.2.cloned.1.call-done, f32[1536]{0:T(1024)S(1)} %copy-done, f32[512]{0:T(512)S(1)} %add_rsqrt_fusion.1), kind=kLoop, calls=%fused_computation.8 | loop fusion | flops 2359296 | bytes 4726784 | tf_op jit(solution)/shard_map/convert_element_type | solution.py:29
  59.5 0.0 copy-done.1
  59.5 1.4 multiply_convert_fusion.1
  60.9 1.5 pad_maximum_fusion.2
  62.3 0.0 all-gather.2.cloned.1.call-update
  62.4 0.5 multiply_cosine_fusion
  62.9 1.2 fusion.8
  64.1 0.6 pad_maximum_fusion.3
  64.8 12.7 %all-gather.2.cloned.1.call-done = bf16[1024,2048]{0,1:T(8,128)(2,1)} async-done(((bf16[512,2048]{0,1:T(8,128)(2,1)}), bf16[1024,2048]{0,1:T(8,128)(2,1)}) %all-gather.2.cloned.1.call-update) | async-done | bytes 4194320 | tf_op jit(solution)/shard_map/all_gather | solution.py:60
  77.5 26.4 %fusion = f32[1024,6144]{0,1:T(8,128)} fusion(bf16[1536,6144]{1,0:T(8,128)(2,1)} %param.12, bf16[1024,2048]{0,1:T(8,128)(2,1)} %all-gather.2.cloned.1.call-done), kind=kOutput, calls=%fused_computation.6 | convolution fusion | flops 19327352832 | bytes 47185920 | tf_op jit(solution)/shard_map/dot_general | solution.py:62
  103.8 6.6 %slice.69 = bf16[1024,32,128]{0,2,1:T(8,128)(2,1)S(1)} slice(f32[1024,32,192]{0,2,1:T(8,128)} %bitcast.9), slice={[0:1024], [0:32], [0:128]} | slice | bytes 16777216 | tf_op jit(solution)/shard_map/slice | solution.py:66
  110.4 4.9 %subtract_convert_fusion = (bf16[1024,32,32]{0,2,1:T(8,128)(2,1)S(1)}, bf16[1024,32,32]{0,2,1:T(8,128)(2,1)S(1)}) fusion(f32[1024,32,192]{0,2,1:T(8,128)} %bitcast.10, f32[1024,32]{0,1:T(8,128)S(1)} %get-tuple-element.17, f32[1024,32]{0,1:T(8,128)S(1)} %get-tuple-element.16), kind=kLoop, calls=%fused_computation.5 | loop fusion | flops 8388608 | bytes 12845056 | tf_op jit(solution)/shard_map/convert.3
  115.3 10.1 %pad_maximum_fusion = bf16[1024,32,192]{0,2,1:T(8,128)(2,1)} fusion(bf16[1024,32,32]{0,2,1:T(8,128)(2,1)S(1)} %get-tuple-element.13, bf16[1024,32,32]{0,2,1:T(8,128)(2,1)S(1)} %get-tuple-element.12, bf16[1024,32,128]{0,2,1:T(8,128)(2,1)S(1)} %slice.69), kind=kLoop, calls=%fused_computation.2 | loop fusion | flops 37748736 | bytes 25165824 | tf_op jit(solution)/shard_map/concatenate | solution.py:66
  125.4 16.6 %copy.18 = bf16[1024,6144]{1,0:T(8,128)(2,1)} copy(bf16[1024,6144]{0,1:T(8,128)(2,1)} %bitcast.8) | data formatting | bytes 25165824
  142.0 15.0 %convolution_convert_fusion = bf16[1024,8192]{1,0:T(8,128)(2,1)} fusion(bf16[512,8192]{1,0:T(8,128)(2,1)} %param.13, bf16[1024,2048]{0,1:T(8,128)(2,1)} %all-gather.2.cloned.1.call-done), kind=kOutput, calls=%fused_computation.1 | convolution fusion | flops 8598323200 | bytes 26214400 | tf_op jit(solution)/shard_map/dot_general | solution.py:68
  (5 shorter events, 0.0 us)
Async XLA Ops:
  7.2 46.6 %reduce-scatter.2.cloned.1.call-start = ((), (), s32[]{:S(2)}) async-start(), calls=%async_computation.1 | async-start | bytes 12976128 | tf_op jit(solution)/shard_map/reduce_scatter | solution.py:41
  7.2 16.7 %copy-start.2 = (bf16[3584,576]{0,1:T(8,128)(2,1)S(1)}, bf16[3584,576]{0,1:T(8,128)(2,1)}, u32[]{:S(2)}) copy-start(bf16[3584,576]{0,1:T(8,128)(2,1)} %param.9) | copy-start | bytes 12386308
  35.3 22.0 %copy-start = (f32[1536]{0:T(1024)S(1)}, f32[1536]{0:T(1024)}, u32[]{:S(2)}) copy-start(f32[1536]{0:T(1024)} %param.10) | copy-start | bytes 18436
  35.3 24.2 %copy-start.1 = (f32[512]{0:T(512)S(1)}, f32[512]{0:T(512)}, u32[]{:S(2)}) copy-start(f32[512]{0:T(512)} %param.11) | copy-start | bytes 6148
  35.3 42.2 %all-gather.2.cloned.1.call-start = ((), (), s32[]{:S(2)}) async-start(), calls=%async_computation.2 | async-start | bytes 6291456 | tf_op jit(solution)/shard_map/all_gather | solution.py:60
Sparse Core Ops, SparseCore 0:
  35.4 18.2 reduce-scatter.1
  62.5 14.9 all-gather.1
where the time goes:
time: 166 us; the launch traced here: 164 us
  matrix products  64.8 us (39%)
  waiting for transfers between devices  30.9 us (19%)
  other arithmetic  30.6 us (18%)
  local copies, waits for them, and re-layouts  23.2 us (14%)
  between operations  14.1 us (8%)
    dot_general x1, matrix products, shards(): jnp.dot(piece[:, :q_width], w_uq, preferred_element_type=jnp.float32)  26.4 us
    reduce_scatter x1, waiting for transfers between devices, shards(): lax.psum_scatter(jnp.concatenate([jnp.dot(hidden, w_dq, preferred_element...  18.2 us
    dot_general x1, matrix products, shards(): jnp.dot(hidden, w_dq, preferred_element_type=jnp.float32)  16.7 us
    unnamed x7, local copies, waits for them, and re-layouts  16.6 us
    dot_general x1, matrix products, shards(): jnp.dot(piece[:, q_width:], w_ukv, preferred_element_type=jnp.float32)  15 us
    all_gather x1, waiting for transfers between devices, shards(): piece = lax.all_gather(latent, 'tensor', axis=0, tiled=True)  12.7 us
    concatenate x1, other arithmetic, shards(): query_out = jnp.concatenate([query_full[:, :, :NOPE], turned], axis=2)  10.1 us
    dot_general x1, matrix products, shards(): jnp.dot(hidden, w_dkv, preferred_element_type=jnp.float32)  6.72 us
  transfers between devices with their start and end apart: 2, of which 2 were waited for; matrix products, arithmetic and copies ran while one was open for 1% of the time, Pallas kernels for 0%

commit v1 on v0

v1 whole, which is shorter than its diff:
```python
import functools

import jax
import jax.numpy as jnp
import numpy as np
from jax import lax
from jax.experimental import pallas as pl
from jax.experimental.pallas import tpu as pltpu
from jax.sharding import PartitionSpec as P

NOPE = 128
ROPE = 64
CHUNKS = 4
HEADS_PER_STEP = 4
F32 = jnp.float32
BF16 = jnp.bfloat16


def table(count, half):
    freqs = np.float32(50000.0) ** (-np.arange(half, dtype=np.float32) / np.float32(half))
    angle = np.arange(count, dtype=np.float32)[:, None] * freqs.astype(np.float32)[None, :]
    angle = angle.astype(np.float64)
    both = np.concatenate([np.cos(angle), np.sin(angle)], axis=1).astype(np.float32)
    return np.concatenate([both, both], axis=1)


def down_kernel(
    hidden_hbm, w_dq_hbm, w_dkv_t_hbm, q_gain, kv_gain,
    q_lat, kv_lat, key_sum,
    hidden, w_q, w_kv, acc, key_acc, send, recv, key_send, key_recv,
    hid_sem, w_sem, send_sem, recv_sem,
):
    me = lax.axis_index("tensor")
    other = 1 - me
    rows = hidden.shape[0]
    width = acc.shape[2]
    q_blocks = w_q.shape[0]
    blocks = q_blocks + 1
    part = rows // CHUNKS
    share = key_recv.shape[1]
    across = (((1,), (1,)), ((), ()))

    def load_hidden(m):
        at = pl.ds(m * part, part)
        return pltpu.make_async_copy(hidden_hbm.at[at], hidden.at[at], hid_sem.at[m])

    def load_w(n):
        if n < q_blocks:
            return pltpu.make_async_copy(
                w_dq_hbm.at[:, pl.ds(n * width, width)], w_q.at[n], w_sem.at[n]
            )
        return pltpu.make_async_copy(w_dkv_t_hbm, w_kv, w_sem.at[n])

    def exchange(n):
        return pltpu.make_async_remote_copy(
            src_ref=send.at[n], dst_ref=recv.at[n],
            send_sem=send_sem.at[n], recv_sem=recv_sem.at[n],
            device_id={"tensor": other}, device_id_type=pl.DeviceIdType.MESH,
        )

    load_hidden(0).start()
    load_w(0).start()
    for m in range(1, CHUNKS):
        load_hidden(m).start()
    for n in range(1, blocks):
        load_w(n).start()

    barrier = pltpu.get_barrier_semaphore()
    pl.semaphore_signal(
        barrier, inc=1, device_id={"tensor": other}, device_id_type=pl.DeviceIdType.MESH
    )
    pl.semaphore_wait(barrier, 1)

    def gather(n):
        total = acc[n] + recv[n].astype(F32)
        acc[n] = total
        return jnp.sum(total * total, axis=1, keepdims=True)

    load_w(0).wait()
    for m in range(CHUNKS):
        load_hidden(m).wait()
        at = pl.ds(m * part, part)
        piece = jnp.dot(hidden[at], w_q[0], preferred_element_type=F32)
        acc[0, at] = piece
        send[0, at] = piece.astype(BF16)
    exchange(0).start()

    squares = None
    for n in range(1, blocks):
        load_w(n).wait()
        if n >= 2:
            exchange(n - 2).wait_recv()
        if n < q_blocks:
            piece = jnp.dot(hidden[...], w_q[n], preferred_element_type=F32)
        else:
            piece = lax.dot_general(
                hidden[...], w_kv[:width], across, preferred_element_type=F32
            )
        acc[n] = piece
        send[n] = piece.astype(BF16)
        if n >= 2:
            more = gather(n - 2)
            squares = more if squares is None else squares + more
        exchange(n).start()

    exchange(q_blocks - 1).wait_recv()
    piece = lax.dot_general(
        w_kv[width:], hidden[...], across, preferred_element_type=F32
    )
    key_acc[...] = piece
    key_send[...] = piece.astype(BF16)
    more = gather(q_blocks - 1)
    squares = more if squares is None else squares + more
    scale = lax.rsqrt(squares / (q_blocks * width) + 1e-06)
    for n in range(q_blocks):
        at = pl.ds(n * width, width)
        q_lat[:, at] = (acc[n] * scale * q_gain[at][None, :]).astype(BF16)
    key_copy = pltpu.make_async_remote_copy(
        src_ref=key_send.at[:, pl.ds(pl.multiple_of(other * share, share), share)], dst_ref=key_recv,
        send_sem=send_sem.at[blocks], recv_sem=recv_sem.at[blocks],
        device_id={"tensor": other}, device_id_type=pl.DeviceIdType.MESH,
    )
    key_copy.start()

    exchange(q_blocks).wait_recv()
    total = acc[q_blocks] + recv[q_blocks].astype(F32)
    scale = lax.rsqrt(jnp.mean(total * total, axis=1, keepdims=True) + 1e-06)
    kv_lat[...] = (total * scale * kv_gain[...][None, :]).astype(BF16)
    key_copy.wait_recv()
    key_sum[...] = key_acc[:, pl.ds(pl.multiple_of(me * share, share), share)] + key_recv[...].astype(F32)
    for n in range(blocks):
        exchange(n).wait_send()
    key_copy.wait_send()


def down(hidden, w_dq, w_dkv, q_gain, kv_gain):
    rows, depth = hidden.shape
    q_width = w_dq.shape[1]
    width = kv_gain.shape[0]
    rope_width = w_dkv.shape[1] - width
    q_blocks = q_width // width
    blocks = q_blocks + 1
    share = rows // lax.axis_size("tensor")
    vmem = pl.BlockSpec(memory_space=pltpu.VMEM)
    hbm = pl.BlockSpec(memory_space=pl.ANY)
    return pl.pallas_call(
        down_kernel,
        out_shape=(
            jax.ShapeDtypeStruct((rows, q_width), BF16),
            jax.ShapeDtypeStruct((rows, width), BF16),
            jax.ShapeDtypeStruct((rope_width, share), F32),
        ),
        in_specs=[hbm, hbm, hbm, vmem, vmem],
        out_specs=(vmem, vmem, vmem),
        scratch_shapes=[
            pltpu.VMEM((rows, depth), BF16),
            pltpu.VMEM((q_blocks, depth, width), BF16),
            pltpu.VMEM((width + rope_width, depth), BF16),
            pltpu.VMEM((blocks, rows, width), F32),
            pltpu.VMEM((rope_width, rows), F32),
            pltpu.VMEM((blocks, rows, width), BF16),
            pltpu.VMEM((blocks, rows, width), BF16),
            pltpu.VMEM((rope_width, rows), BF16),
            pltpu.VMEM((rope_width, share), BF16),
            pltpu.SemaphoreType.DMA((CHUNKS,)),
            pltpu.SemaphoreType.DMA((blocks,)),
            pltpu.SemaphoreType.DMA((blocks + 1,)),
            pltpu.SemaphoreType.DMA((blocks + 1,)),
        ],
        compiler_params=pltpu.CompilerParams(
            collective_id=0, has_side_effects=True, vmem_limit_bytes=60 * 1024 * 1024
        ),
        name="down",
    )(hidden, w_dq, w_dkv.T, q_gain, kv_gain)


def up_kernel(q_lat, kv_lat, key_sum, key_tab, tab, w_uq, w_ukv, queries, keys_values, rotary_key, cosine, sine):
    half = ROPE // 2
    lanes = 2 * ROPE
    lane = lax.broadcasted_iota(jnp.int32, (1, lanes), 1)
    first = lane % ROPE < half

    @pl.when(pl.program_id(0) == 0)
    def _():
        both = tab[...]
        cosine[...] = jnp.where(first, both, pltpu.roll(both, half, 1))
        sine[...] = jnp.where(first, -pltpu.roll(both, lanes - half, 1), both)
        one, two = key_sum[:half], key_sum[half:]
        share = key_sum.shape[1]
        own = pl.ds(pl.multiple_of(lax.axis_index("tensor") * share, share), share)
        cos, sin = key_tab[:half, own], key_tab[half:, own]
        rotary_key[:half] = (one * cos - two * sin).astype(BF16)
        rotary_key[half:] = (two * cos + one * sin).astype(BF16)

    full = jnp.dot(q_lat[...], w_uq[...], preferred_element_type=F32)
    low = lane < ROPE
    pair = 2 * (NOPE + ROPE)
    for start in range(0, full.shape[1], pair):
        one = full[:, start + NOPE : start + 2 * NOPE]
        two = full[:, start + 2 * NOPE : start + pair]
        rope = jnp.where(low, one, two)
        swapped = jnp.where(
            first, pltpu.roll(rope, lanes - half, 1), pltpu.roll(rope, half, 1)
        )
        turned = rope * cosine[...] + swapped * sine[...]
        queries[:, start : start + NOPE] = full[:, start : start + NOPE].astype(BF16)
        queries[:, start + NOPE : start + 2 * NOPE] = jnp.where(low, turned, one).astype(BF16)
        queries[:, start + 2 * NOPE : start + pair] = jnp.where(low, two, turned).astype(BF16)
    keys_values[...] = jnp.dot(
        kv_lat[...], w_ukv[...], preferred_element_type=F32
    ).astype(BF16)


def up(q_lat, kv_lat, key_sum, key_tab, tab, w_uq, w_ukv):
    rows, q_width = q_lat.shape
    width = kv_lat.shape[1]
    q_cols = HEADS_PER_STEP * (NOPE + ROPE)
    steps = w_uq.shape[1] // q_cols
    kv_cols = w_ukv.shape[1] // steps
    fixed = lambda *shape: pl.BlockSpec(shape, lambda i: (0, 0))
    moving = lambda *shape: pl.BlockSpec(shape, lambda i: (0, i))
    return pl.pallas_call(
        up_kernel,
        grid=(steps,),
        out_shape=(
            jax.ShapeDtypeStruct((rows, w_uq.shape[1]), BF16),
            jax.ShapeDtypeStruct((rows, w_ukv.shape[1]), BF16),
            jax.ShapeDtypeStruct(key_sum.shape, BF16),
        ),
        in_specs=[
            fixed(rows, q_width),
            fixed(rows, width),
            fixed(*key_sum.shape),
            fixed(*key_tab.shape),
            fixed(*tab.shape),
            moving(q_width, q_cols),
            moving(width, kv_cols),
        ],
        out_specs=(moving(rows, q_cols), moving(rows, kv_cols), fixed(*key_sum.shape)),
        scratch_shapes=[pltpu.VMEM(tab.shape, F32), pltpu.VMEM(tab.shape, F32)],
        compiler_params=pltpu.CompilerParams(
            dimension_semantics=("arbitrary",), vmem_limit_bytes=60 * 1024 * 1024
        ),
        name="up",
    )(q_lat, kv_lat, key_sum, key_tab, tab, w_uq, w_ukv)


def normalize(block, gain):
    scale = lax.rsqrt(jnp.mean(block * block, axis=1, keepdims=True) + 1e-06)
    return (block * scale * gain[None, :]).astype(BF16)


def down_any(hidden, w_dq, w_dkv, q_gain, kv_gain):
    q_width = w_dq.shape[1]
    kv_end = q_width + kv_gain.shape[0]
    partial = jnp.concatenate(
        [
            jnp.dot(hidden, w_dq, preferred_element_type=F32),
            jnp.dot(hidden, w_dkv, preferred_element_type=F32),
        ],
        axis=1,
    )
    own = lax.psum_scatter(partial, "tensor", scatter_dimension=0, tiled=True)
    latent = jnp.concatenate(
        [normalize(own[:, :q_width], q_gain), normalize(own[:, q_width:kv_end], kv_gain)],
        axis=1,
    )
    latent = lax.all_gather(latent, "tensor", axis=0, tiled=True)
    return latent[:, :q_width], latent[:, q_width:], own[:, kv_end:].T


def shards(hidden, w_dq, w_dkv, q_gain, kv_gain, w_uq, w_ukv):
    project = down if lax.axis_size("tensor") == 2 else down_any
    q_lat, kv_lat, key_sum = project(hidden, w_dq, w_dkv, q_gain, kv_gain)
    tab = table(hidden.shape[0], ROPE // 2)
    key_tab = jnp.asarray(tab[:, :ROPE].T)
    queries, keys_values, rotary_key = up(
        q_lat, kv_lat, key_sum, key_tab, jnp.asarray(tab), w_uq, w_ukv
    )
    return queries, keys_values, rotary_key.T


def solution(mesh):
    in_specs = (
        P("dp", "tensor"),
        P("tensor", None),
        P("tensor", None),
        P(),
        P(),
        P(None, "tensor"),
        P(None, "tensor"),
    )
    out_specs = (P("dp", "tensor"), P("dp", "tensor"), P(("dp", "tensor"), None))
    return jax.shard_map(shards, mesh=mesh, in_specs=in_specs, out_specs=out_specs, check_vma=False)
```

time: 166 us -> 62.9 us (0.38); the launches traced: 164 us -> 62.7 us
  matrix products: 64.8 us -> 0 us
  Pallas kernels: 0 us -> 62 us
  waiting for transfers between devices: 30.9 us -> 0 us
  other arithmetic: 30.6 us -> 0 us
  local copies, waits for them, and re-layouts: 23.2 us -> 0 us
  between operations: 14.1 us -> 0.64 us
    dot_general x4 -> x0, matrix products: 64.8 us -> none  [the longest x1 26.4 us: shards(): jnp.dot(piece[:, :q_width], w_uq, preferred_element_type=jnp.float32)]
    pallas_call x0 -> x2, Pallas kernels: none -> 62 us  [the longest x1 35.2 us: up(): pl.pallas_call(up_kernel, grid=(steps,), out_shape=(jax.ShapeDtypeStruct(...]
    reduce_scatter x1 -> x0, waiting for transfers between devices: 18.2 us -> none  [shards(): lax.psum_scatter(jnp.concatenate([jnp.dot(hidden, w_dq, preferred_element...]
    concatenate x4 -> x0, other arithmetic: 16.8 us -> none  [the longest x1 10.1 us: shards(): query_out = jnp.concatenate([query_full[:, :, :NOPE], turned], axis=2)]
    unnamed x7 -> x0, local copies, waits for them, and re-layouts: 16.6 us -> none
    all_gather x1 -> x0, waiting for transfers between devices: 12.7 us -> none  [shards(): piece = lax.all_gather(latent, 'tensor', axis=0, tiled=True)]
    slice x1 -> x0, local copies, waits for them, and re-layouts: 6.59 us -> none  [shards(): query_out = jnp.concatenate([query_full[:, :, :NOPE], turned], axis=2)]
    another operation x2 -> x0, other arithmetic: 6.07 us -> none
  transfers between devices with their start and end apart: 2 -> 0, of which waited for: 2 -> 0; matrix products, arithmetic and copies ran while one was open for 1% -> 0% of each run, Pallas kernels for 0% -> 0%
where the time goes in v1:
time: 62.9 us; the launch traced here: 62.7 us
  Pallas kernels  62 us (99%)
  between operations  0.64 us (1%)
    pallas_call x1, Pallas kernels, up(): pl.pallas_call(up_kernel, grid=(steps,), out_shape=(jax.ShapeDtypeStruct(...  35.2 us
    pallas_call x1, Pallas kernels, down(): pl.pallas_call(down_kernel, out_shape=(jax.ShapeDtypeStruct((rows, q_widt...  26.8 us

profile of v1, /device:TPU:13, one launch (start us, length us, event | category | flops | bytes accessed | tf_op | source)
XLA Modules:
  0.0 62.7 jit_solution(10584117198213729069)
XLA Ops:
  0.6 26.8 %down.1 = (bf16[1024,1536]{1,0:T(8,128)(2,1)}, bf16[1024,512]{1,0:T(8,128)(2,1)}, f32[64,512]{1,0:T(8,128)}) custom-call(bf16[1024,3584]{1,0:T(8,128)(2,1)} %hidden_hbm.1, bf16[3584,1536]{1,0:T(8,128)(2,1)} %w_dq_hbm.1, bf16[576,3584]{1,0:T(8,128)(2,1)} %bitcast.2, f32[1536]{0:T(1024)} %q_gain.1, f32[512]{0:T(512)} %kv_gain.1), custom_call_target="tpu_custom_call" | custom-call | tf_op jit(solution)/shard_map/down/pallas_call | solution.py:146
  27.4 35.2 %up.1 = (bf16[1024,6144]{1,0:T(8,128)(2,1)}, bf16[1024,8192]{1,0:T(8,128)(2,1)}, bf16[64,512]{1,0:T(8,128)(2,1)}) custom-call(bf16[1024,1536]{1,0:T(8,128)(2,1)} %get-tuple-element.9.q_lat, bf16[1024,512]{1,0:T(8,128)(2,1)} %get-tuple-element.10.kv_lat, f32[64,512]{1,0:T(8,128)} %get-tuple-element.11.key_sum, f32[64,1024]{1,0:T(8,128)} %constant.4.clone.key_tab, ...), custom_call_target="tpu_custom_call" | custom-call | tf_op jit(solution)/shard_map/up/pallas_call | solution.py:222

commit v2 on v1

--- a/solution.py
+++ b/solution.py
@@ -168,7 +168,7 @@
             pltpu.SemaphoreType.DMA((blocks + 1,)),
         ],
         compiler_params=pltpu.CompilerParams(
-            collective_id=0, has_side_effects=True, vmem_limit_bytes=60 * 1024 * 1024
+            collective_id=0, has_side_effects=True, vmem_limit_bytes=47 * 1024 * 1024
         ),
         name="down",
     )(hidden, w_dq, w_dkv.T, q_gain, kv_gain)
@@ -239,7 +239,7 @@
         out_specs=(moving(rows, q_cols), moving(rows, kv_cols), fixed(*key_sum.shape)),
         scratch_shapes=[pltpu.VMEM(tab.shape, F32), pltpu.VMEM(tab.shape, F32)],
         compiler_params=pltpu.CompilerParams(
-            dimension_semantics=("arbitrary",), vmem_limit_bytes=60 * 1024 * 1024
+            dimension_semantics=("arbitrary",), vmem_limit_bytes=40 * 1024 * 1024
         ),
         name="up",
     )(q_lat, kv_lat, key_sum, key_tab, tab, w_uq, w_ukv)

time: 62.9 us -> 61.3 us (0.975)
  Pallas kernels: 62 us -> 59 us
  local copies, waits for them, and re-layouts: 0 us -> 1.38 us
    pallas_call x1, Pallas kernels: 26.8 us -> 24.2 us  [down(): pl.pallas_call(down_kernel, out_shape=(jax.ShapeDtypeStruct((rows, q_widt...]
    unnamed x0 -> x10, local copies, waits for them, and re-layouts: none -> 1.38 us
where the time goes in v2:
time: 61.3 us; the launch traced here: 61.1 us
  Pallas kernels  59 us (96%)
  local copies, waits for them, and re-layouts  1.38 us (2%)
  between operations  0.68 us (1%)
    pallas_call x1, Pallas kernels, up(): pl.pallas_call(up_kernel, grid=(steps,), out_shape=(jax.ShapeDtypeStruct(...  34.8 us
    pallas_call x1, Pallas kernels, down(): pl.pallas_call(down_kernel, out_shape=(jax.ShapeDtypeStruct((rows, q_widt...  24.2 us
    unnamed x10, local copies, waits for them, and re-layouts  1.38 us

profile of v2, /device:TPU:13, one launch (start us, length us, event | category | flops | bytes accessed | tf_op | source)
XLA Modules:
  0.0 61.1 jit_solution(3570715935467607976)
XLA Ops:
  0.6 0.0 copy-start.3
  0.6 0.7 %copy-done.3 = f32[1536]{0:T(1024)S(1)} copy-done((f32[1536]{0:T(1024)S(1)}, f32[1536]{0:T(1024)}, u32[]{:S(2)}) %copy-start.3) | copy-done | bytes 6168
  1.3 0.0 copy-start.4
  1.3 0.7 %copy-done.4 = f32[512]{0:T(512)S(1)} copy-done((f32[512]{0:T(512)S(1)}, f32[512]{0:T(512)}, u32[]{:S(2)}) %copy-start.4) | copy-done | bytes 2072
  2.0 0.0 copy-start
  2.0 0.0 copy-start.1
  2.0 0.0 copy-start.2
  2.0 24.2 %down.1 = (bf16[1024,1536]{1,0:T(8,128)(2,1)S(1)}, bf16[1024,512]{1,0:T(8,128)(2,1)S(1)}, f32[64,512]{1,0:T(8,128)S(1)}) custom-call(bf16[1024,3584]{1,0:T(8,128)(2,1)} %hidden_hbm.1, bf16[3584,1536]{1,0:T(8,128)(2,1)} %w_dq_hbm.1, bf16[576,3584]{1,0:T(8,128)(2,1)} %bitcast.2, f32[1536]{0:T(1024)S(1)} %copy-done.3, f32[512]{0:T(512)S(1)} %copy-done.4), custom_call_target="tpu_custom_call" | custom-call | tf_op jit(solution)/shard_map/down/pallas_call | solution.py:146
  26.2 0.0 copy-done
  26.2 0.0 copy-done.1
  26.2 0.0 copy-done.2
  26.2 34.8 %up.1 = (bf16[1024,6144]{1,0:T(8,128)(2,1)}, bf16[1024,8192]{1,0:T(8,128)(2,1)}, bf16[64,512]{1,0:T(8,128)(2,1)}) custom-call(bf16[1024,1536]{1,0:T(8,128)(2,1)S(1)} %get-tuple-element.9.q_lat, bf16[1024,512]{1,0:T(8,128)(2,1)S(1)} %get-tuple-element.10.kv_lat, f32[64,512]{1,0:T(8,128)S(1)} %get-tuple-element.11.key_sum, f32[64,1024]{1,0:T(8,128)S(1)} %copy-done.2, ...), custom_call_target="tpu_custom_call" | custom-call | tf_op jit(solution)/shard_map/up/pallas_call | solution.py:222
Async XLA Ops:
  0.6 0.7 %copy-start.3 = (f32[1536]{0:T(1024)S(1)}, f32[1536]{0:T(1024)}, u32[]{:S(2)}) copy-start(f32[1536]{0:T(1024)} %q_gain.1) | copy-start | bytes 18436
  1.3 0.7 %copy-start.4 = (f32[512]{0:T(512)S(1)}, f32[512]{0:T(512)}, u32[]{:S(2)}) copy-start(f32[512]{0:T(512)} %kv_gain.1) | copy-start | bytes 6148
  2.0 24.2 %copy-start = (bf16[512,8192]{1,0:T(8,128)(2,1)S(1)}, bf16[512,8192]{1,0:T(8,128)(2,1)}, u32[]{:S(2)}) copy-start(bf16[512,8192]{1,0:T(8,128)(2,1)} %w_ukv.1) | copy-start | bytes 25165828
  2.0 24.2 %copy-start.1 = (f32[1024,128]{1,0:T(8,128)S(1)}, f32[1024,128]{1,0:T(8,128)}, u32[]{:S(2)}) copy-start(f32[1024,128]{1,0:T(8,128)} %constant.5.clone.tab) | copy-start | bytes 1572868
  2.0 24.2 %copy-start.2 = (f32[64,1024]{1,0:T(8,128)S(1)}, f32[64,1024]{1,0:T(8,128)}, u32[]{:S(2)}) copy-start(f32[64,1024]{1,0:T(8,128)} %constant.4.clone.key_tab) | copy-start | bytes 786436
